TPU v7x, 512 devices: a whole 4x8x8 slice. The times are simulated.
512 devices in a mesh: sub: 64 (over x, y_lo, z), agg: 8 (over y_hi, core).
Axes of the slice: x: 4, y: 8 (y_hi: 4, y_lo: 2; y = y_hi * 2 + y_lo), z: 8, core: 2. Of those that a mesh axis runs over, the one named last changes fastest.
Arguments:
- block_values: float32 [7, 4, 4, 524288], P(None, None, None, ('sub', 'agg'))
- block_cols: int32 [7, 524288], P(None, ('sub', 'agg')), may hold values from 0 to 524287, as said below
- coarse_rhs: float32 [4, 524288], P(None, ('sub', 'agg'))
- guess: float32 [4, 524288], P(None, ('sub', 'agg')), may hold values from -3 to 3
- bound_low: int32 [1], replicated, may hold values from 20 to 26
- bound_high: int32 [1], replicated, may hold values from 32 to 40
Outputs:
- smoothed: float32 [4, 524288], P(None, ('sub', 'agg'))
- residual: float32 [4, 524288], P(None, ('sub', 'agg'))
- residual_rms: float32 [1], replicated
Inputs may be any that keep to these rules, and one draw needn't show every extreme that they name: Block rows form 524288 / 1024 planes of 1024 consecutive rows, in a periodic order. block_cols[0] is the row itself, block_cols[1] a row of the previous plane, block_cols[2] a row of the next plane, block_cols[3] to block_cols[6] rows of the same plane.
All inputs are finite; a program needn't handle non-finite values.
Results may differ from a plain program's by a relative error of at most 0.0001.
Values sent between devices are 32-bit elements; how exact they have to be, the bound alone decides.
A program may use at most 64 MiB of HBM per device.

v0:
```python
import jax
import jax.numpy as jnp
from jax import lax
from jax.experimental import pallas as pl
from jax.experimental.pallas import tpu as pltpu
from jax.sharding import Mesh
from jax.sharding import PartitionSpec as P

STEPS = 4
COMP = 4
BLOCKS = 7
AXES = ("x", "yl", "z", "yh", "c")
SIZES = (4, 2, 8, 4, 2)
MESH_ID = pl.DeviceIdType.MESH


def plane_device(plane):
    coords = []
    for size in reversed(SIZES):
        coords.append(lax.rem(plane, size))
        plane = lax.div(plane, size)
    return tuple(reversed(coords))


def own_plane():
    plane = lax.axis_index(AXES[0])
    for name, size in zip(AXES[1:], SIZES[1:]):
        plane = plane * size + lax.axis_index(name)
    return plane


def smoother(values_hbm, cols_hbm, rhs_hbm, guess_hbm, low_hbm, high_hbm,
             smoothed_hbm, residual_hbm, square_hbm,
             values, cols, packed, low, high, sent, below, above, shown, square,
             load_sem, store_sem, below_send, below_recv, above_send, above_recv):
    planes = 1
    for size in SIZES:
        planes *= size
    me = own_plane()
    prev_dev = plane_device(lax.rem(me + planes - 1, planes))
    next_dev = plane_device(lax.rem(me + 1, planes))

    barrier = pltpu.get_barrier_semaphore()
    pl.semaphore_signal(barrier, inc=1, device_id=prev_dev, device_id_type=MESH_ID)
    pl.semaphore_signal(barrier, inc=1, device_id=next_dev, device_id_type=MESH_ID)

    loads = [
        pltpu.make_async_copy(guess_hbm, packed.at[0], load_sem.at[0]),
        pltpu.make_async_copy(low_hbm, low, load_sem.at[1]),
        pltpu.make_async_copy(high_hbm, high, load_sem.at[2]),
        pltpu.make_async_copy(cols_hbm, cols, load_sem.at[3]),
        pltpu.make_async_copy(rhs_hbm, packed.at[1], load_sem.at[4]),
        pltpu.make_async_copy(values_hbm, values, load_sem.at[5]),
    ]
    for load in loads:
        load.start()

    def unpack(ref):
        return [ref[pl.ds(c, 8, stride=COMP), :] for c in range(COMP)]

    def exchange(slot):
        copies = [
            pltpu.make_async_remote_copy(
                sent.at[slot], below.at[slot], below_send.at[slot], below_recv.at[slot],
                device_id=next_dev, device_id_type=MESH_ID),
            pltpu.make_async_remote_copy(
                sent.at[slot], above.at[slot], above_send.at[slot], above_recv.at[slot],
                device_id=prev_dev, device_id_type=MESH_ID),
        ]
        for copy in copies:
            copy.start()
        return copies

    loads[0].wait()
    field = unpack(packed.at[0])
    for c in range(COMP):
        sent[0, c] = field[c]
    pl.semaphore_wait(barrier, 2)
    copies = exchange(0)

    loads[1].wait()
    loads[2].wait()
    lower = jnp.full((8, 128), low[0], jnp.int32).astype(jnp.float32) / 4.0
    upper = jnp.full((8, 128), high[0], jnp.int32).astype(jnp.float32) / 4.0
    centre = (upper + lower) / 2.0
    half_width = (upper - lower) / 2.0
    spread_ratio = centre / half_width
    ratio = 1.0 / spread_ratio

    loads[3].wait()
    lanes, masks = {}, {}
    for k in range(1, BLOCKS):
        index = jnp.concatenate([cols[k:k + 1, t * 128:(t + 1) * 128] for t in range(8)], axis=0)
        lanes[k] = index & 127
        masks[k] = [(index & (128 << b)) != 0 for b in range(3)]

    def taken(ref, c, k):
        parts = []
        for t in range(8):
            chunk = jnp.broadcast_to(ref[c, t:t + 1, :], (8, 128))
            parts.append(jnp.take_along_axis(chunk, lanes[k], axis=1, mode="promise_in_bounds"))
        for b in range(3):
            parts = [jnp.where(masks[k][b], parts[2 * i + 1], parts[2 * i]) for i in range(len(parts) // 2)]
        return parts[0]

    def add_block(total, k, column, gathered):
        for i in range(COMP):
            block = values[k, i, pl.ds(column, 8, stride=COMP), :]
            total[i] = total[i] - block * gathered

    def subtract_own(residual, field, slot):
        total = list(residual)
        for j in range(COMP):
            add_block(total, 0, j, field[j])
        for k in range(3, BLOCKS):
            for j in range(COMP):
                add_block(total, k, j, taken(sent.at[slot], j, k))
        return total

    def subtract_far(total, slot):
        total = list(total)
        for k, ref in ((1, below), (2, above)):
            for j in range(COMP):
                add_block(total, k, j, taken(ref.at[slot], j, k))
        return total

    loads[4].wait()
    loads[5].wait()
    smoothed = field
    residual = unpack(packed.at[1])
    pending = []
    direction = field
    for slot in range(STEPS + 1):
        residual = subtract_own(residual, direction, slot)
        for copy in copies:
            copy.wait_recv()
        pending += copies
        residual = subtract_far(residual, slot)
        if slot == 0:
            direction = [r / centre for r in residual]
        elif slot < STEPS:
            following = 1.0 / (2.0 * spread_ratio - ratio)
            keep = following * ratio
            gain = 2.0 * following / half_width
            direction = [keep * d + gain * r for d, r in zip(direction, residual)]
            ratio = following
        if slot < STEPS:
            for c in range(COMP):
                sent[slot + 1, c] = direction[c]
            copies = exchange(slot + 1)
            smoothed = [s + d for s, d in zip(smoothed, direction)]
    for c in range(COMP):
        shown[0, pl.ds(c, 8, stride=COMP), :] = smoothed[c]
        shown[1, pl.ds(c, 8, stride=COMP), :] = residual[c]
    square[...] = sum(r * r for r in residual)
    stores = [
        pltpu.make_async_copy(shown.at[0], smoothed_hbm, store_sem.at[0]),
        pltpu.make_async_copy(shown.at[1], residual_hbm, store_sem.at[1]),
        pltpu.make_async_copy(square, square_hbm, store_sem.at[2]),
    ]
    for store in stores:
        store.start()
    for copy in pending:
        copy.wait_send()
    for store in stores:
        store.wait()


def shards(block_values, block_cols, coarse_rhs, guess, bound_low, bound_high):
    rows = block_values.shape[3]

    def packed_rows(a):
        lead = a.shape[:-2]
        a = a.reshape(*lead, COMP, rows // 128, 128)
        return jnp.swapaxes(a, -3, -2).reshape(*lead, COMP * rows // 128, 128)

    def unpacked_rows(a):
        return jnp.swapaxes(a.reshape(rows // 128, COMP, 128), 0, 1).reshape(COMP, rows)

    def hbm():
        return pl.BlockSpec(memory_space=pl.ANY)

    slots = STEPS + 1
    field = jax.ShapeDtypeStruct((32, 128), jnp.float32)
    smoothed, residual, square = pl.pallas_call(
        smoother,
        out_shape=(field, field, jax.ShapeDtypeStruct((8, 128), jnp.float32)),
        in_specs=[hbm()] * 6,
        out_specs=(hbm(),) * 3,
        scratch_shapes=[
            pltpu.VMEM((BLOCKS, COMP, 32, 128), jnp.float32),
            pltpu.VMEM((BLOCKS, rows), jnp.int32),
            pltpu.VMEM((2, 32, 128), jnp.float32),
            pltpu.SMEM((1,), jnp.int32),
            pltpu.SMEM((1,), jnp.int32),
            pltpu.VMEM((slots, COMP, 8, 128), jnp.float32),
            pltpu.VMEM((slots, COMP, 8, 128), jnp.float32),
            pltpu.VMEM((slots, COMP, 8, 128), jnp.float32),
            pltpu.VMEM((2, 32, 128), jnp.float32),
            pltpu.VMEM((8, 128), jnp.float32),
            pltpu.SemaphoreType.DMA((6,)),
            pltpu.SemaphoreType.DMA((3,)),
            pltpu.SemaphoreType.DMA((slots,)),
            pltpu.SemaphoreType.DMA((slots,)),
            pltpu.SemaphoreType.DMA((slots,)),
            pltpu.SemaphoreType.DMA((slots,)),
        ],
        compiler_params=pltpu.CompilerParams(collective_id=0, has_side_effects=True),
        name="smoother",
    )(packed_rows(block_values), block_cols, packed_rows(coarse_rhs), packed_rows(guess), bound_low, bound_high)
    total_sq = lax.psum(jnp.sum(square), AXES)
    count = COMP * rows * lax.axis_size(AXES)
    rms = jnp.sqrt(total_sq / (1.0 * count) + 1e-06).reshape(1)
    return unpacked_rows(smoothed), unpacked_rows(residual), rms


def solution(mesh):
    finer = Mesh(mesh.devices.reshape(SIZES), AXES)
    return jax.shard_map(
        shards,
        mesh=finer,
        in_specs=(
            P(None, None, None, AXES),
            P(None, AXES),
            P(None, AXES),
            P(None, AXES),
            P(),
            P(),
        ),
        out_specs=(P(None, AXES), P(None, AXES), P()),
        check_vma=False,
    )
```

profile of v0, /device:TPU:1, one launch (start us, length us, event | category | flops | bytes accessed | tf_op | source)
XLA Modules:
  0.0 143.5 jit_solution(280797705985927096)
XLA Ops:
  1.9 38.1 %smoother.1 = (f32[32,128]{1,0:T(8,128)}, f32[32,128]{1,0:T(8,128)}, f32[8,128]{1,0:T(8,128)}) custom-call(f32[7,4,32,128]{3,2,1,0:T(8,128)} %bitcast.26, s32[7,1024]{1,0:T(8,128)} %cols_hbm.1, f32[32,128]{1,0:T(8,128)} %bitcast.27, f32[32,128]{1,0:T(8,128)} %bitcast.28, s32[1]{0:T(128)S(6)} %copy.16.low_hbm, s32[1]{0:T(128)S(6)} %copy.17.high_hbm), custom_call_target="tpu_custom_call" | custom-call | tf_op jit(solution)/shard_map/smoother/pallas_call | solution.py:185
  40.0 0.0 copy-start.1
  40.1 1.3 reduce_sum.9
  41.3 99.0 %psum.7 = f32[]{:T(128)} all-reduce(f32[]{:T(128)} %reduce_sum.9), channel_id=1, replica_groups=mesh['x'=4,'yl'=2,'z'=8,'yh'=4,'c'=2] {'x','yl','z','yh','c'}, use_global_device_ids=true, to_apply=%region_1.0 | all-reduce | flops 1 | bytes 8 | tf_op jit(solution)/shard_map/psum | solution.py:211
  141.0 0.0 copy-done.1
  141.0 0.0 copy-start
  141.0 0.6 copy.18
  141.6 0.1 copy-done
  141.7 0.6 copy.19
Async XLA Ops:
  40.0 100.9 %copy-start.1 = (f32[32,128]{1,0:T(8,128)S(1)}, f32[32,128]{1,0:T(8,128)}, u32[]{:S(2)}) copy-start(f32[32,128]{1,0:T(8,128)} %get-tuple-element.6) | copy-start | bytes 49156
  141.0 0.7 copy-start
where the time goes:
time: 144 us; the launch traced here: 143 us
  blocking collectives  99 us (69%)
  Pallas kernels  38.1 us (26%)
  between operations  3.78 us (3%)
    psum x1, blocking collectives, shards(): total_sq = lax.psum(jnp.sum(square), AXES)  99 us
    pallas_call x1, Pallas kernels, shards(): pl.pallas_call(smoother, out_shape=(field, field, jax.ShapeDtypeStruct((8...  38.1 us

commit v1 on v0

--- a/solution.py
+++ b/solution.py
@@ -30,9 +30,10 @@
 
 
 def smoother(values_hbm, cols_hbm, rhs_hbm, guess_hbm, low_hbm, high_hbm,
-             smoothed_hbm, residual_hbm, square_hbm,
-             values, cols, packed, low, high, sent, below, above, shown, square,
-             load_sem, store_sem, below_send, below_recv, above_send, above_recv):
+             smoothed_hbm, residual_hbm, rms_out,
+             values, cols, packed, low, high, sent, below, above, shown, partial, line, sheet,
+             load_sem, store_sem, below_send, below_recv, above_send, above_recv,
+             line_send, line_recv, sheet_send, sheet_recv, ready):
     planes = 1
     for size in SIZES:
         planes *= size
@@ -40,9 +41,32 @@
     prev_dev = plane_device(lax.rem(me + planes - 1, planes))
     next_dev = plane_device(lax.rem(me + 1, planes))
 
+    x, yl, z, yh, core = (lax.axis_index(name) for name in AXES)
+    y = yh * 2 + yl
+
+    def on_line(step):
+        other = lax.rem(z * 2 + core + step, 16)
+        return x, yl, lax.div(other, 2), yh, lax.rem(other, 2)
+
+    def on_sheet(step):
+        other = lax.rem(x * 8 + y + step, 32)
+        other_y = lax.rem(other, 8)
+        return lax.div(other, 8), lax.rem(other_y, 2), z, lax.div(other_y, 2), core
+
+    def on_row(step):
+        other_y = lax.rem(y + step, 8)
+        return x, lax.rem(other_y, 2), z, lax.div(other_y, 2), core
+
+    def on_column(step):
+        return lax.rem(x + step, 4), yl, z, yh, core
+
+    greeted = [prev_dev, next_dev]
+    greeted += [on_line(step) for step in range(1, 16)]
+    greeted += [on_row(step) for step in range(1, 8)]
+    greeted += [on_column(step) for step in range(1, 4)]
     barrier = pltpu.get_barrier_semaphore()
-    pl.semaphore_signal(barrier, inc=1, device_id=prev_dev, device_id_type=MESH_ID)
-    pl.semaphore_signal(barrier, inc=1, device_id=next_dev, device_id_type=MESH_ID)
+    for device in greeted:
+        pl.semaphore_signal(barrier, inc=1, device_id=device, device_id_type=MESH_ID)
 
     loads = [
         pltpu.make_async_copy(guess_hbm, packed.at[0], load_sem.at[0]),
@@ -75,8 +99,10 @@
     field = unpack(packed.at[0])
     for c in range(COMP):
         sent[0, c] = field[c]
-    pl.semaphore_wait(barrier, 2)
+    pl.semaphore_wait(barrier, len(greeted))
     copies = exchange(0)
+    for step in range(1, 8):
+        pl.semaphore_signal(ready, inc=1, device_id=on_row(step), device_id_type=MESH_ID)
 
     loads[1].wait()
     loads[2].wait()
@@ -152,14 +178,39 @@
     for c in range(COMP):
         shown[0, pl.ds(c, 8, stride=COMP), :] = smoothed[c]
         shown[1, pl.ds(c, 8, stride=COMP), :] = residual[c]
-    square[...] = sum(r * r for r in residual)
     stores = [
         pltpu.make_async_copy(shown.at[0], smoothed_hbm, store_sem.at[0]),
         pltpu.make_async_copy(shown.at[1], residual_hbm, store_sem.at[1]),
-        pltpu.make_async_copy(square, square_hbm, store_sem.at[2]),
     ]
+    squares = jnp.sum(sum(r * r for r in residual), axis=0, keepdims=True)
+
+    def spread(value, slots, own, device, peers, send_sem, recv_sem):
+        partial[...] = value
+        slots[own] = value
+        sends = []
+        for step in range(1, peers):
+            send = pltpu.make_async_remote_copy(
+                partial, slots.at[own], send_sem, recv_sem,
+                device_id=device(step), device_id_type=MESH_ID)
+            send.start()
+            sends.append(send)
+        arrived = slots.at[pl.ds(0, peers - 1)]
+        pltpu.make_async_copy(arrived, arrived, recv_sem).wait()
+        total = slots[0]
+        for peer in range(1, peers):
+            total = total + slots[peer]
+        pltpu.make_async_copy(arrived, arrived, send_sem).wait()
+        return total
+
+    squares = spread(squares, line, z * 2 + core, on_line, 16, line_send, line_recv)
     for store in stores:
         store.start()
+    pl.semaphore_wait(ready, 7)
+    squares = spread(squares, sheet, x * 8 + y, on_sheet, 32, sheet_send, sheet_recv)
+    total = jnp.sum(squares, axis=1, keepdims=True)
+    entries = planes * COMP * 8 * 128
+    rms = jnp.sqrt(total / (1.0 * entries) + 1e-06)
+    rms_out[0] = rms[0, 0]
     for copy in pending:
         copy.wait_send()
     for store in stores:
@@ -178,15 +229,15 @@
         return jnp.swapaxes(a.reshape(rows // 128, COMP, 128), 0, 1).reshape(COMP, rows)
 
     def hbm():
-        return pl.BlockSpec(memory_space=pl.ANY)
+        return pl.BlockSpec(memory_space=pltpu.HBM)
 
     slots = STEPS + 1
     field = jax.ShapeDtypeStruct((32, 128), jnp.float32)
-    smoothed, residual, square = pl.pallas_call(
+    smoothed, residual, rms = pl.pallas_call(
         smoother,
-        out_shape=(field, field, jax.ShapeDtypeStruct((8, 128), jnp.float32)),
+        out_shape=(field, field, jax.ShapeDtypeStruct((1,), jnp.float32)),
         in_specs=[hbm()] * 6,
-        out_specs=(hbm(),) * 3,
+        out_specs=(hbm(), hbm(), pl.BlockSpec(memory_space=pltpu.SMEM)),
         scratch_shapes=[
             pltpu.VMEM((BLOCKS, COMP, 32, 128), jnp.float32),
             pltpu.VMEM((BLOCKS, rows), jnp.int32),
@@ -197,20 +248,24 @@
             pltpu.VMEM((slots, COMP, 8, 128), jnp.float32),
             pltpu.VMEM((slots, COMP, 8, 128), jnp.float32),
             pltpu.VMEM((2, 32, 128), jnp.float32),
-            pltpu.VMEM((8, 128), jnp.float32),
+            pltpu.VMEM((1, 128), jnp.float32),
+            pltpu.VMEM((16, 1, 128), jnp.float32),
+            pltpu.VMEM((32, 1, 128), jnp.float32),
             pltpu.SemaphoreType.DMA((6,)),
-            pltpu.SemaphoreType.DMA((3,)),
-            pltpu.SemaphoreType.DMA((slots,)),
-            pltpu.SemaphoreType.DMA((slots,)),
-            pltpu.SemaphoreType.DMA((slots,)),
-            pltpu.SemaphoreType.DMA((slots,)),
+            pltpu.SemaphoreType.DMA((2,)),
+            pltpu.SemaphoreType.DMA((slots,)),
+            pltpu.SemaphoreType.DMA((slots,)),
+            pltpu.SemaphoreType.DMA((slots,)),
+            pltpu.SemaphoreType.DMA((slots,)),
+            pltpu.SemaphoreType.DMA,
+            pltpu.SemaphoreType.DMA,
+            pltpu.SemaphoreType.DMA,
+            pltpu.SemaphoreType.DMA,
+            pltpu.SemaphoreType.REGULAR,
         ],
         compiler_params=pltpu.CompilerParams(collective_id=0, has_side_effects=True),
         name="smoother",
     )(packed_rows(block_values), block_cols, packed_rows(coarse_rhs), packed_rows(guess), bound_low, bound_high)
-    total_sq = lax.psum(jnp.sum(square), AXES)
-    count = COMP * rows * lax.axis_size(AXES)
-    rms = jnp.sqrt(total_sq / (1.0 * count) + 1e-06).reshape(1)
     return unpacked_rows(smoothed), unpacked_rows(residual), rms
 
 

time: 144 us -> 54.3 us (0.38)
  blocking collectives: 99 us -> 0 us
  Pallas kernels: 38.1 us -> 48.3 us
    psum x1 -> x0, blocking collectives: 99 us -> none  [shards(): total_sq = lax.psum(jnp.sum(square), AXES)]
    pallas_call x1, Pallas kernels: 38.1 us -> 48.3 us  [shards(): pl.pallas_call(smoother, out_shape=(field, field, jax.ShapeDtypeStruct((1...]
where the time goes in v1:
time: 54.3 us; the launch traced here: 53.9 us
  Pallas kernels  48.3 us (89%)
  between operations  3.68 us (7%)
  local copies, waits for them, and re-layouts  1.94 us (4%)
    pallas_call x1, Pallas kernels, shards(): pl.pallas_call(smoother, out_shape=(field, field, jax.ShapeDtypeStruct((1...  48.3 us
    unnamed x4, local copies, waits for them, and re-layouts  1.94 us

profile of v1, /device:TPU:1, one launch (start us, length us, event | category | flops | bytes accessed | tf_op | source)
XLA Modules:
  0.0 53.9 jit_solution(3040236195654183438)
XLA Ops:
  1.9 48.3 %smoother.1 = (f32[32,128]{1,0:T(8,128)}, f32[32,128]{1,0:T(8,128)}, f32[1]{0:T(128)}) custom-call(f32[7,4,32,128]{3,2,1,0:T(8,128)} %bitcast.25, s32[7,1024]{1,0:T(8,128)} %cols_hbm.1, f32[32,128]{1,0:T(8,128)} %bitcast.26, f32[32,128]{1,0:T(8,128)} %bitcast.27, s32[1]{0:T(128)S(6)} %copy.17.low_hbm, s32[1]{0:T(128)S(6)} %copy.18.high_hbm), custom_call_target="tpu_custom_call" | custom-call | tf_op jit(solution)/shard_map/smoother/pallas_call | solution.py:236
  50.3 0.0 copy-start
  50.3 1.3 %copy.19 = f32[4,1024]{1,0:T(4,128)} copy(f32[4,1024]{1,0:T(4,128)} %bitcast.29) | data formatting | bytes 32768
  51.6 0.0 copy-done
  51.6 0.6 %copy.20 = f32[4,1024]{1,0:T(4,128)} copy(f32[4,1024]{1,0:T(4,128)S(1)} %bitcast.28) | data formatting | bytes 32768
Async XLA Ops:
  50.3 1.3 %copy-start = (f32[32,128]{1,0:T(8,128)S(1)}, f32[32,128]{1,0:T(8,128)}, u32[]{:S(2)}) copy-start(f32[32,128]{1,0:T(8,128)} %get-tuple-element.7) | copy-start | bytes 49156
